TPU v7x, 32 devices: a whole 2x2x4 slice. The times are simulated.
32 devices in a mesh: row: 4 (over y, x), col: 8 (over z, core).
Axes of the slice: x: 2, y: 2, z: 4, core: 2. Of those that a mesh axis runs over, the one named last changes fastest.
Arguments:
- right_side: bfloat16 [4, 8, 8, 128, 256], P('row', 'col'), may hold values from -6 to 6
- diag_inverse: bfloat16 [4, 8, 8, 128, 128], P('row', 'col'), may hold values from -0.5 to 0.5
- panels: bfloat16 [7, 4, 400, 128, 128], P(None, 'row', 'col'), may hold values from -0.0546875 to 0.0546875
- tile_source: int32 [7, 4, 400], P(None, 'row', 'col'), may hold values from 0 to 3
- tile_target: int32 [7, 4, 400], P(None, 'row', 'col'), may hold values from 0 to 7
Outputs:
- solution: float32 [4, 8, 8, 128, 256], P('row', 'col')
All inputs are finite; a program needn't handle non-finite values.
Results may differ from a plain program's by a relative error of at most 0.017.
Values may be sent and summed in bfloat16 or wider, within the bound.
No kernel may reach another device: no remote copies, remote signals or barrier semaphores. Data moves between devices by JAX's collectives and lax.ppermute only.
A program may use at most 128 MiB of HBM per device.

v0:
```python
import jax
import jax.numpy as jnp
from jax import lax
from jax.sharding import PartitionSpec as P


def local_update(segment, panel, source, target):
    columns = lax.axis_size("col")
    picked = jnp.take(segment, source, axis=0)
    prods = jnp.einsum("qab,qbc->qac", panel, picked, preferred_element_type=jnp.float32)
    onehot = (target[None, :] == jnp.arange(columns, dtype=jnp.int32)[:, None]).astype(jnp.float32)
    sums = jnp.dot(onehot, prods.reshape(prods.shape[0], -1), precision=lax.Precision.HIGHEST)
    return sums.reshape(columns, prods.shape[1], prods.shape[2]).astype(jnp.bfloat16)


def advance_whole(block, panel, source, target):
    segment = lax.all_gather(block.astype(jnp.bfloat16)[None], "row", axis=0, tiled=True)
    partial_value = local_update(segment, panel, source, target)
    return lax.psum_scatter(partial_value, "col", scatter_dimension=0, tiled=True).astype(
        jnp.float32
    )[0]


def local(right_side, diag_inverse, panels, tile_source, tile_target):
    sections = right_side.shape[2]
    width = right_side.shape[4]
    bounds = [(0, width)]
    incoming = [None for bound in bounds]
    solved = []
    for section in range(sections):
        lower, upper = bounds[0]
        current = right_side[0, 0, section, :, lower:upper].astype(jnp.float32)
        if section > 0:
            current = current - incoming[0]
        block = jnp.dot(
            diag_inverse[0, 0, section],
            current.astype(jnp.bfloat16),
            preferred_element_type=jnp.float32,
        )
        if section + 1 < sections:
            incoming[0] = advance_whole(
                block, panels[section, 0], tile_source[section, 0], tile_target[section, 0]
            )
        solved.append(block)
    return jnp.stack(solved, axis=0)[None, None]


def solution(mesh):
    return jax.shard_map(
        local,
        mesh=mesh,
        in_specs=(
            P("row", "col", None, None, None),
            P("row", "col", None, None, None),
            P(None, "row", "col", None, None),
            P(None, "row", "col"),
            P(None, "row", "col"),
        ),
        out_specs=P("row", "col", None, None, None),
        check_vma=False,
    )
```

profile of v0, /device:TPU:0, one launch (start us, length us, event | category | flops | bytes accessed | tf_op | source)
XLA Modules:
  0.0 471.4 jit_solution(18376820517892712203)
XLA Ops:
  6.5 1.7 bitcast_dynamic-update-slice_fusion.6
  8.2 10.5 %all-gather = bf16[512,256]{1,0:T(8,128)(2,1)S(1)} all-gather(bf16[128,256]{1,0:T(8,128)(2,1)S(1)} %get-tuple-element.40), channel_id=2, replica_groups=mesh['row'=4,'col'=8] {'row'}, dimensions={0}, use_global_device_ids=true | all-gather | bytes 327680 | tf_op jit(solution)/shard_map/all_gather | solution.py:17
  18.7 1.4 compare_and_fusion
  20.8 5.3 %fusion.35 = f32[50,128,256]{1,2,0:T(8,128)} fusion(bf16[50,128,256]{2,1,0:T(8,128)(2,1)S(1)} %gather_fusion, pred[50]{0:T(512)(128)(4,1)S(1)} %get-tuple-element.35, bf16[7,1,50,128,128]{4,3,2,1,0:T(8,128)(2,1)} %param.9), kind=kOutput, calls=%fused_computation.49 | convolution fusion | flops 421068800 | bytes 11468850 | tf_op jit(solution)/shard_map/qab,qbc->qac/dot_general | solution.py:10
  26.1 8.2 %copy.56 = f32[50,128,256]{2,1,0:T(8,128)} copy(f32[50,128,256]{1,2,0:T(8,128)} %fusion.35) | data formatting | bytes 13107200 | tf_op jit(solution)/shard_map/qab,qbc->qac/dot_general | solution.py:10
  34.3 3.3 slice_bitcast_fusion.6
  38.1 6.1 %fusion.77 = bf16[8,128,256]{2,0,1:T(8,128)(2,1)S(1)} fusion(f32[128,256,50]{1,0,2:T(8,128)S(1)} %slice_bitcast_fusion.6, s32[50]{0:T(128)S(1)} %get-tuple-element.25), kind=kOutput, calls=%fused_computation.77 | convolution fusion | flops 157548944 | bytes 7078088 | tf_op jit(solution)/shard_map/dot_general | solution.py:12
  44.2 0.9 copy.58
  45.2 31.7 %reduce-scatter.8.cloned.1.call-done = bf16[1,128,256]{2,1,0:T(8,128)(2,1)} async-done(((bf16[8,128,256]{2,1,0:T(8,128)(2,1)}), bf16[1,128,256]{2,1,0:T(8,128)(2,1)}) %reduce-scatter.8.cloned.1.call-update) | async-done | bytes 65552 | tf_op jit(solution)/shard_map/reduce_scatter | solution.py:19
  76.9 1.7 bitcast_dynamic-update-slice_fusion.5
  78.6 9.0 %all-gather.1 = bf16[512,256]{1,0:T(8,128)(2,1)S(1)} all-gather(bf16[128,256]{1,0:T(8,128)(2,1)S(1)} %bitcast.364), channel_id=3, replica_groups=mesh['row'=4,'col'=8] {'row'}, dimensions={0}, use_global_device_ids=true | all-gather | bytes 327680 | tf_op jit(solution)/shard_map/all_gather | solution.py:17
  87.7 0.8 gather_fusion.1
  88.4 5.3 %fusion.38 = f32[50,128,256]{1,2,0:T(8,128)} fusion(bf16[50,128,256]{2,1,0:T(8,128)(2,1)S(1)} %gather_fusion.1, pred[50]{0:T(512)(128)(4,1)} %get-tuple-element.33, bf16[7,1,50,128,128]{4,3,2,1,0:T(8,128)(2,1)} %param.9), kind=kOutput, calls=%fused_computation.50 | convolution fusion | flops 421068800 | bytes 11469312 | tf_op jit(solution)/shard_map/qab,qbc->qac/dot_general | solution.py:10
  93.7 8.2 %copy.61 = f32[50,128,256]{2,1,0:T(8,128)} copy(f32[50,128,256]{1,2,0:T(8,128)} %fusion.38) | data formatting | bytes 13107200 | tf_op jit(solution)/shard_map/qab,qbc->qac/dot_general | solution.py:10
  101.9 3.3 slice_bitcast_fusion.5
  105.2 6.1 %fusion.80 = bf16[8,128,256]{2,0,1:T(8,128)(2,1)S(1)} fusion(f32[128,256,50]{1,0,2:T(8,128)S(1)} %slice_bitcast_fusion.5, s32[50]{0:T(128)S(1)} %copy-done.3), kind=kOutput, calls=%fused_computation.78 | convolution fusion | flops 157548944 | bytes 7078088 | tf_op jit(solution)/shard_map/dot_general | solution.py:12
  111.3 0.9 copy.63
  112.3 28.8 %reduce-scatter.10.cloned.1.call-done = bf16[1,128,256]{2,1,0:T(8,128)(2,1)} async-done(((bf16[8,128,256]{2,1,0:T(8,128)(2,1)}), bf16[1,128,256]{2,1,0:T(8,128)(2,1)}) %reduce-scatter.10.cloned.1.call-update) | async-done | bytes 65552 | tf_op jit(solution)/shard_map/reduce_scatter | solution.py:19
  141.1 1.7 bitcast_dynamic-update-slice_fusion.4
  142.8 9.5 %all-gather.2 = bf16[512,256]{1,0:T(8,128)(2,1)S(1)} all-gather(bf16[128,256]{1,0:T(8,128)(2,1)S(1)} %bitcast.365), channel_id=4, replica_groups=mesh['row'=4,'col'=8] {'row'}, dimensions={0}, use_global_device_ids=true | all-gather | bytes 327680 | tf_op jit(solution)/shard_map/all_gather | solution.py:17
  152.3 0.8 gather_fusion.2
  153.0 5.3 %fusion.41 = f32[50,128,256]{1,2,0:T(8,128)} fusion(bf16[50,128,256]{2,1,0:T(8,128)(2,1)S(1)} %gather_fusion.2, pred[50]{0:T(512)(128)(4,1)} %get-tuple-element.31, bf16[7,1,50,128,128]{4,3,2,1,0:T(8,128)(2,1)} %param.9), kind=kOutput, calls=%fused_computation.51 | convolution fusion | flops 421068800 | bytes 11469312 | tf_op jit(solution)/shard_map/qab,qbc->qac/dot_general | solution.py:10
  158.3 8.2 %copy.66 = f32[50,128,256]{2,1,0:T(8,128)} copy(f32[50,128,256]{1,2,0:T(8,128)} %fusion.41) | data formatting | bytes 13107200 | tf_op jit(solution)/shard_map/qab,qbc->qac/dot_general | solution.py:10
  166.5 3.3 slice_bitcast_fusion.4
  169.8 6.1 %fusion.83 = bf16[8,128,256]{2,0,1:T(8,128)(2,1)S(1)} fusion(f32[128,256,50]{1,0,2:T(8,128)S(1)} %slice_bitcast_fusion.4, s32[50]{0:T(128)S(1)} %copy-done.2), kind=kOutput, calls=%fused_computation.79 | convolution fusion | flops 157548944 | bytes 7078088 | tf_op jit(solution)/shard_map/dot_general | solution.py:12
  175.9 0.9 copy.68
  176.9 28.7 %reduce-scatter.12.cloned.1.call-done = bf16[1,128,256]{2,1,0:T(8,128)(2,1)} async-done(((bf16[8,128,256]{2,1,0:T(8,128)(2,1)}), bf16[1,128,256]{2,1,0:T(8,128)(2,1)}) %reduce-scatter.12.cloned.1.call-update) | async-done | bytes 65552 | tf_op jit(solution)/shard_map/reduce_scatter | solution.py:19
  205.7 1.7 bitcast_dynamic-update-slice_fusion.3
  207.4 8.9 %all-gather.3 = bf16[512,256]{1,0:T(8,128)(2,1)S(1)} all-gather(bf16[128,256]{1,0:T(8,128)(2,1)S(1)} %bitcast.366), channel_id=5, replica_groups=mesh['row'=4,'col'=8] {'row'}, dimensions={0}, use_global_device_ids=true | all-gather | bytes 327680 | tf_op jit(solution)/shard_map/all_gather | solution.py:17
  216.3 0.8 gather_fusion.3
  217.1 5.3 %fusion.44 = f32[50,128,256]{1,2,0:T(8,128)} fusion(bf16[50,128,256]{2,1,0:T(8,128)(2,1)S(1)} %gather_fusion.3, pred[50]{0:T(512)(128)(4,1)} %get-tuple-element.29, bf16[7,1,50,128,128]{4,3,2,1,0:T(8,128)(2,1)} %param.9), kind=kOutput, calls=%fused_computation.52 | convolution fusion | flops 421068800 | bytes 11469312 | tf_op jit(solution)/shard_map/qab,qbc->qac/dot_general | solution.py:10
  222.4 8.2 %copy.71 = f32[50,128,256]{2,1,0:T(8,128)} copy(f32[50,128,256]{1,2,0:T(8,128)} %fusion.44) | data formatting | bytes 13107200 | tf_op jit(solution)/shard_map/qab,qbc->qac/dot_general | solution.py:10
  230.6 3.3 slice_bitcast_fusion.3
  233.9 6.1 %fusion.86 = bf16[8,128,256]{2,0,1:T(8,128)(2,1)S(1)} fusion(f32[128,256,50]{1,0,2:T(8,128)S(1)} %slice_bitcast_fusion.3, s32[50]{0:T(128)S(1)} %copy-done.1), kind=kOutput, calls=%fused_computation.80 | convolution fusion | flops 157548944 | bytes 7078088 | tf_op jit(solution)/shard_map/dot_general | solution.py:12
  240.0 0.9 copy.73
  241.0 28.8 %reduce-scatter.14.cloned.1.call-done = bf16[1,128,256]{2,1,0:T(8,128)(2,1)} async-done(((bf16[8,128,256]{2,1,0:T(8,128)(2,1)}), bf16[1,128,256]{2,1,0:T(8,128)(2,1)}) %reduce-scatter.14.cloned.1.call-update) | async-done | bytes 65552 | tf_op jit(solution)/shard_map/reduce_scatter | solution.py:19
  269.8 1.7 bitcast_dynamic-update-slice_fusion.2
  271.5 9.3 %all-gather.4 = bf16[512,256]{1,0:T(8,128)(2,1)S(1)} all-gather(bf16[128,256]{1,0:T(8,128)(2,1)S(1)} %bitcast.367), channel_id=6, replica_groups=mesh['row'=4,'col'=8] {'row'}, dimensions={0}, use_global_device_ids=true | all-gather | bytes 327680 | tf_op jit(solution)/shard_map/all_gather | solution.py:17
  280.8 0.8 gather_fusion.4
  281.6 5.3 %fusion.47 = f32[50,128,256]{1,2,0:T(8,128)} fusion(bf16[50,128,256]{2,1,0:T(8,128)(2,1)S(1)} %gather_fusion.4, pred[50]{0:T(512)(128)(4,1)} %get-tuple-element.27, bf16[7,1,50,128,128]{4,3,2,1,0:T(8,128)(2,1)} %param.9), kind=kOutput, calls=%fused_computation.53 | convolution fusion | flops 421068800 | bytes 11469312 | tf_op jit(solution)/shard_map/qab,qbc->qac/dot_general | solution.py:10
  286.8 8.2 %copy.76 = f32[50,128,256]{2,1,0:T(8,128)} copy(f32[50,128,256]{1,2,0:T(8,128)} %fusion.47) | data formatting | bytes 13107200 | tf_op jit(solution)/shard_map/qab,qbc->qac/dot_general | solution.py:10
  295.0 3.3 slice_bitcast_fusion.2
  298.3 6.1 %fusion.89 = bf16[8,128,256]{2,0,1:T(8,128)(2,1)S(1)} fusion(f32[128,256,50]{1,0,2:T(8,128)S(1)} %slice_bitcast_fusion.2, s32[50]{0:T(128)S(1)} %get-tuple-element.21), kind=kOutput, calls=%fused_computation.81 | convolution fusion | flops 157548944 | bytes 7078088 | tf_op jit(solution)/shard_map/dot_general | solution.py:12
  304.5 0.9 copy.78
  305.5 28.5 %reduce-scatter.16.cloned.1.call-done = bf16[1,128,256]{2,1,0:T(8,128)(2,1)} async-done(((bf16[8,128,256]{2,1,0:T(8,128)(2,1)}), bf16[1,128,256]{2,1,0:T(8,128)(2,1)}) %reduce-scatter.16.cloned.1.call-update) | async-done | bytes 65552 | tf_op jit(solution)/shard_map/reduce_scatter | solution.py:19
  333.9 1.7 bitcast_dynamic-update-slice_fusion.1
  335.6 9.2 %all-gather.5 = bf16[512,256]{1,0:T(8,128)(2,1)S(1)} all-gather(bf16[128,256]{1,0:T(8,128)(2,1)S(1)} %bitcast.368), channel_id=7, replica_groups=mesh['row'=4,'col'=8] {'row'}, dimensions={0}, use_global_device_ids=true | all-gather | bytes 327680 | tf_op jit(solution)/shard_map/all_gather | solution.py:17
  344.9 0.8 gather_fusion.5
  345.6 5.3 %fusion.50 = f32[50,128,256]{1,2,0:T(8,128)} fusion(bf16[50,128,256]{2,1,0:T(8,128)(2,1)S(1)} %gather_fusion.5, pred[50]{0:T(512)(128)(4,1)S(1)} %copy-done.5, bf16[7,1,50,128,128]{4,3,2,1,0:T(8,128)(2,1)} %param.9), kind=kOutput, calls=%fused_computation.54 | convolution fusion | flops 421068800 | bytes 11468850 | tf_op jit(solution)/shard_map/qab,qbc->qac/dot_general | solution.py:10
  350.9 8.2 %copy.81 = f32[50,128,256]{2,1,0:T(8,128)} copy(f32[50,128,256]{1,2,0:T(8,128)} %fusion.50) | data formatting | bytes 13107200 | tf_op jit(solution)/shard_map/qab,qbc->qac/dot_general | solution.py:10
  359.1 3.3 slice_bitcast_fusion.1
  362.4 6.1 %fusion.92 = bf16[8,128,256]{2,0,1:T(8,128)(2,1)S(1)} fusion(f32[128,256,50]{1,0,2:T(8,128)S(1)} %slice_bitcast_fusion.1, s32[50]{0:T(128)S(1)} %get-tuple-element.26), kind=kOutput, calls=%fused_computation.82 | convolution fusion | flops 157548944 | bytes 7078088 | tf_op jit(solution)/shard_map/dot_general | solution.py:12
  368.5 0.9 copy.83
  369.5 28.6 %reduce-scatter.18.cloned.1.call-done = bf16[1,128,256]{2,1,0:T(8,128)(2,1)} async-done(((bf16[8,128,256]{2,1,0:T(8,128)(2,1)}), bf16[1,128,256]{2,1,0:T(8,128)(2,1)}) %reduce-scatter.18.cloned.1.call-update) | async-done | bytes 65552 | tf_op jit(solution)/shard_map/reduce_scatter | solution.py:19
  398.1 1.7 bitcast_dynamic-update-slice_fusion
  399.8 9.7 %all-gather.6 = bf16[512,256]{1,0:T(8,128)(2,1)S(1)} all-gather(bf16[128,256]{1,0:T(8,128)(2,1)S(1)} %bitcast.369), channel_id=8, replica_groups=mesh['row'=4,'col'=8] {'row'}, dimensions={0}, use_global_device_ids=true | all-gather | bytes 327680 | tf_op jit(solution)/shard_map/all_gather | solution.py:17
  409.5 0.8 gather_fusion.6
  410.3 5.3 %fusion.53 = f32[50,128,256]{1,2,0:T(8,128)} fusion(bf16[50,128,256]{2,1,0:T(8,128)(2,1)S(1)} %gather_fusion.6, pred[50]{0:T(512)(128)(4,1)S(1)} %copy-done.4, bf16[7,1,50,128,128]{4,3,2,1,0:T(8,128)(2,1)} %param.9), kind=kOutput, calls=%fused_computation.55 | convolution fusion | flops 421068800 | bytes 11468850 | tf_op jit(solution)/shard_map/qab,qbc->qac/dot_general | solution.py:10
  415.6 8.2 %copy.86 = f32[50,128,256]{2,1,0:T(8,128)} copy(f32[50,128,256]{1,2,0:T(8,128)} %fusion.53) | data formatting | bytes 13107200 | tf_op jit(solution)/shard_map/qab,qbc->qac/dot_general | solution.py:10
  423.8 3.3 slice_bitcast_fusion
  427.0 6.1 %fusion.95 = bf16[8,128,256]{2,0,1:T(8,128)(2,1)S(1)} fusion(f32[128,256,50]{1,0,2:T(8,128)S(1)} %slice_bitcast_fusion, s32[50]{0:T(128)S(1)} %get-tuple-element.20), kind=kOutput, calls=%fused_computation.83 | convolution fusion | flops 157548944 | bytes 7078088 | tf_op jit(solution)/shard_map/dot_general | solution.py:12
  433.1 0.9 copy.88
  434.1 28.7 %reduce-scatter.20.cloned.1.call-done = bf16[1,128,256]{2,1,0:T(8,128)(2,1)} async-done(((bf16[8,128,256]{2,1,0:T(8,128)(2,1)}), bf16[1,128,256]{2,1,0:T(8,128)(2,1)}) %reduce-scatter.20.cloned.1.call-update) | async-done | bytes 65552 | tf_op jit(solution)/shard_map/reduce_scatter | solution.py:19
  462.8 1.7 fusion.98
  (47 shorter events, 1.7 us)
Async XLA Ops:
  6.5 70.4 %reduce-scatter.8.cloned.1.call-start = ((), (), s32[]{:S(2)}) async-start(), calls=%async_computation.7 | async-start | bytes 589824 | tf_op jit(solution)/shard_map/reduce_scatter | solution.py:19
  34.3 3.3 copy-start
  37.6 7.6 %copy-start.11 = (s32[50]{0:T(128)S(1)}, s32[50]{0:T(128)}, u32[]{:S(2)}) copy-start(s32[50]{0:T(128)} %get-tuple-element.34) | copy-start | bytes 604
  45.2 95.9 %reduce-scatter.10.cloned.1.call-start = ((), (), s32[]{:S(2)}) async-start(), calls=%async_computation.8 | async-start | bytes 589824 | tf_op jit(solution)/shard_map/reduce_scatter | solution.py:19
  101.9 3.3 copy-start.3
  105.2 7.1 %copy-start.10 = (s32[50]{0:T(128)S(1)}, s32[50]{0:T(128)}, u32[]{:S(2)}) copy-start(s32[50]{0:T(128)} %get-tuple-element.32) | copy-start | bytes 604
  112.3 93.4 %reduce-scatter.12.cloned.1.call-start = ((), (), s32[]{:S(2)}) async-start(), calls=%async_computation.9 | async-start | bytes 589824 | tf_op jit(solution)/shard_map/reduce_scatter | solution.py:19
  166.5 3.3 copy-start.2
  169.8 7.1 %copy-start.9 = (s32[50]{0:T(128)S(1)}, s32[50]{0:T(128)}, u32[]{:S(2)}) copy-start(s32[50]{0:T(128)} %get-tuple-element.30) | copy-start | bytes 604
  176.9 92.9 %reduce-scatter.14.cloned.1.call-start = ((), (), s32[]{:S(2)}) async-start(), calls=%async_computation.10 | async-start | bytes 589824 | tf_op jit(solution)/shard_map/reduce_scatter | solution.py:19
  230.6 3.3 copy-start.1
  233.9 7.1 %copy-start.8 = (s32[50]{0:T(128)S(1)}, s32[50]{0:T(128)}, u32[]{:S(2)}) copy-start(s32[50]{0:T(128)} %get-tuple-element.28) | copy-start | bytes 604
  240.9 93.0 %reduce-scatter.16.cloned.1.call-start = ((), (), s32[]{:S(2)}) async-start(), calls=%async_computation.11 | async-start | bytes 589824 | tf_op jit(solution)/shard_map/reduce_scatter | solution.py:19
  298.3 7.1 %copy-start.7 = (s32[50]{0:T(128)S(1)}, s32[50]{0:T(128)}, u32[]{:S(2)}) copy-start(s32[50]{0:T(128)} %get-tuple-element.38) | copy-start | bytes 604
  304.4 41.2 %copy-start.5 = (pred[50]{0:T(512)(128)(4,1)S(1)}, pred[50]{0:T(512)(128)(4,1)}, u32[]{:S(2)}) copy-start(pred[50]{0:T(512)(128)(4,1)} %get-tuple-element.37) | copy-start | bytes 154
  305.4 92.7 %reduce-scatter.18.cloned.1.call-start = ((), (), s32[]{:S(2)}) async-start(), calls=%async_computation.12 | async-start | bytes 589824 | tf_op jit(solution)/shard_map/reduce_scatter | solution.py:19
  362.4 7.1 %copy-start.6 = (s32[50]{0:T(128)S(1)}, s32[50]{0:T(128)}, u32[]{:S(2)}) copy-start(s32[50]{0:T(128)} %get-tuple-element.7) | copy-start | bytes 604
  362.4 47.8 %copy-start.4 = (pred[50]{0:T(512)(128)(4,1)S(1)}, pred[50]{0:T(512)(128)(4,1)}, u32[]{:S(2)}) copy-start(pred[50]{0:T(512)(128)(4,1)} %get-tuple-element.6) | copy-start | bytes 154
  369.5 93.3 %reduce-scatter.20.cloned.1.call-start = ((), (), s32[]{:S(2)}) async-start(), calls=%async_computation.13 | async-start | bytes 589824 | tf_op jit(solution)/shard_map/reduce_scatter | solution.py:19
Sparse Core Ops, SparseCore 0:
  45.3 31.5 reduce-scatter.7
  112.4 28.6 reduce-scatter.9
  177.0 28.6 reduce-scatter.11
  241.1 28.6 reduce-scatter.13
  305.5 28.3 reduce-scatter.15
  369.6 28.4 reduce-scatter.17
  434.2 28.5 reduce-scatter.19
where the time goes:
time: 480 us; the launch traced here: 471 us
  waiting for transfers between devices  204 us (42%)
  matrix products  93.2 us (19%)
  local copies, waits for them, and re-layouts  92.6 us (19%)
  blocking collectives  66.1 us (14%)
  between operations  14 us (3%)
    reduce_scatter x7, waiting for transfers between devices, advance_whole(): lax.psum_scatter(partial_value, 'col', scatter_dimension=0, tiled=True)  204 us
    all_gather x7, blocking collectives, advance_whole(): lax.all_gather(block.astype(jnp.bfloat16)[None], 'row', axis=0, tiled=True)  66.1 us
    dot_general x7, local copies, waits for them, and re-layouts, local_update(): jnp.einsum('qab,qbc->qac', panel, picked, preferred_element_type=jnp.floa...  57.4 us
    dot_general x7, matrix products, local_update(): jnp.dot(onehot, prods.reshape(prods.shape[0], -1), precision=lax.Precisio...  42.7 us
    dot_general x7, matrix products, local_update(): jnp.einsum('qab,qbc->qac', panel, picked, preferred_element_type=jnp.floa...  37 us
    dot_general x7, local copies, waits for them, and re-layouts, local_update(): jnp.dot(onehot, prods.reshape(prods.shape[0], -1), precision=lax.Precisio...  23 us
    dot_general x8, matrix products, local(): jnp.dot(diag_inverse[0, 0, section], current.astype(jnp.bfloat16), prefer...  13.5 us
  transfers between devices with their start and end apart: 7, of which 7 were waited for; matrix products, arithmetic and copies ran while one was open for 0% of the time, Pallas kernels for 0%

commit v1 on v0

--- a/solution.py
+++ b/solution.py
@@ -2,6 +2,11 @@
 import jax.numpy as jnp
 from jax import lax
 from jax.sharding import PartitionSpec as P
+
+
+def gather_by_exchange(value, axis, dim):
+    copies = jnp.concatenate([value] * lax.axis_size(axis), axis=dim)
+    return lax.all_to_all(copies, axis, dim, dim, tiled=True)
 
 
 def local_update(segment, panel, source, target):
@@ -14,7 +19,7 @@
 
 
 def advance_whole(block, panel, source, target):
-    segment = lax.all_gather(block.astype(jnp.bfloat16)[None], "row", axis=0, tiled=True)
+    segment = gather_by_exchange(block.astype(jnp.bfloat16)[None], "row", 0)
     partial_value = local_update(segment, panel, source, target)
     return lax.psum_scatter(partial_value, "col", scatter_dimension=0, tiled=True).astype(
         jnp.float32

time: 480 us -> 484 us (level)
  blocking collectives: 66.1 us -> 0 us
  waiting for transfers between devices: 204 us -> 238 us
  starting transfers between devices: 0.25 us -> 28.8 us
  local copies, waits for them, and re-layouts: 92.6 us -> 98.2 us
    all_gather x7 -> x0, blocking collectives: 66.1 us -> none  [advance_whole(): lax.all_gather(block.astype(jnp.bfloat16)[None], 'row', axis=0, tiled=True)]
    all_to_all x0 -> x7, waiting for transfers between devices: none -> 33.1 us  [gather_by_exchange(): return lax.all_to_all(copies, axis, dim, dim, tiled=True)]
    all_to_all x0 -> x7, starting transfers between devices: none -> 27.2 us  [gather_by_exchange(): return lax.all_to_all(copies, axis, dim, dim, tiled=True)]
    concatenate x0 -> x7, local copies, waits for them, and re-layouts: none -> 4.96 us  [gather_by_exchange(): copies = jnp.concatenate([value] * lax.axis_size(axis), axis=dim)]
  transfers between devices with their start and end apart: 7 -> 14, of which waited for: 7 -> 14; matrix products, arithmetic and copies ran while one was open for 0% -> 1% of each run, Pallas kernels for 0% -> 0%
where the time goes in v1:
time: 484 us; the launch traced here: 475 us
  waiting for transfers between devices  238 us (49%)
  local copies, waits for them, and re-layouts  98.2 us (20%)
  matrix products  93.6 us (19%)
  starting transfers between devices  28.8 us (6%)
  between operations  14.3 us (3%)
    reduce_scatter x7, waiting for transfers between devices, advance_whole(): lax.psum_scatter(partial_value, 'col', scatter_dimension=0, tiled=True)  205 us
    dot_general x7, local copies, waits for them, and re-layouts, local_update(): jnp.einsum('qab,qbc->qac', panel, picked, preferred_element_type=jnp.floa...  57.4 us
    dot_general x7, matrix products, local_update(): jnp.dot(onehot, prods.reshape(prods.shape[0], -1), precision=lax.Precisio...  42.7 us
    dot_general x7, matrix products, local_update(): jnp.einsum('qab,qbc->qac', panel, picked, preferred_element_type=jnp.floa...  37.3 us
    all_to_all x7, waiting for transfers between devices, gather_by_exchange(): return lax.all_to_all(copies, axis, dim, dim, tiled=True)  33.1 us
    all_to_all x7, starting transfers between devices, gather_by_exchange(): return lax.all_to_all(copies, axis, dim, dim, tiled=True)  27.2 us
    dot_general x7, local copies, waits for them, and re-layouts, local_update(): jnp.dot(onehot, prods.reshape(prods.shape[0], -1), precision=lax.Precisio...  23 us
    dot_general x8, matrix products, local(): jnp.dot(diag_inverse[0, 0, section], current.astype(jnp.bfloat16), prefer...  13.5 us
  transfers between devices with their start and end apart: 14, of which 14 were waited for; matrix products, arithmetic and copies ran while one was open for 1% of the time, Pallas kernels for 0%

profile of v1, /device:TPU:0, one launch (start us, length us, event | category | flops | bytes accessed | tf_op | source)
XLA Modules:
  0.0 474.6 jit_solution(8009915956248128005)
XLA Ops:
  6.5 1.7 bitcast_dynamic-update-slice_fusion.6
  8.9 5.2 %all-to-all-start = ((bf16[4,128,256]{2,1,0:T(8,128)(2,1)}), bf16[4,128,256]{2,1,0:T(8,128)(2,1)S(1)}, u32[]{:S(2)}, u32[]{:S(2)}) async-start(bf16[4,128,256]{2,1,0:T(8,128)(2,1)} %concatenate.21), calls=%async_computation | async-start | bytes 524288 | tf_op jit(solution)/shard_map/all_to_all | solution.py:9
  14.1 1.4 compare_and_fusion
  15.5 1.4 slice_bitcast_fusion.7
  16.9 2.6 all-to-all-done
  20.2 5.3 %fusion.35 = f32[50,128,256]{1,2,0:T(8,128)} fusion(bf16[50,128,256]{2,1,0:T(8,128)(2,1)S(1)} %gather_fusion, pred[50]{0:T(512)(128)(4,1)} %get-tuple-element.35, bf16[7,1,50,128,128]{4,3,2,1,0:T(8,128)(2,1)} %param.9), kind=kOutput, calls=%fused_computation.49 | convolution fusion | flops 421068800 | bytes 11469312 | tf_op jit(solution)/shard_map/qab,qbc->qac/dot_general | solution.py:15
  25.6 8.2 %copy.56 = f32[50,128,256]{2,1,0:T(8,128)} copy(f32[50,128,256]{1,2,0:T(8,128)} %fusion.35) | data formatting | bytes 13107200 | tf_op jit(solution)/shard_map/qab,qbc->qac/dot_general | solution.py:15
  33.8 3.3 slice_bitcast_fusion.6
  37.1 6.1 %fusion.77 = bf16[8,128,256]{2,0,1:T(8,128)(2,1)S(1)} fusion(f32[128,256,50]{1,0,2:T(8,128)S(1)} %slice_bitcast_fusion.6, s32[50]{0:T(128)S(1)} %copy-done.3), kind=kOutput, calls=%fused_computation.77 | convolution fusion | flops 157548944 | bytes 7078088 | tf_op jit(solution)/shard_map/dot_general | solution.py:17
  43.2 0.9 copy.58
  44.1 31.5 %reduce-scatter.8.cloned.1.call-done = bf16[1,128,256]{2,1,0:T(8,128)(2,1)} async-done(((bf16[8,128,256]{2,1,0:T(8,128)(2,1)}), bf16[1,128,256]{2,1,0:T(8,128)(2,1)}) %reduce-scatter.8.cloned.1.call-update) | async-done | bytes 65552 | tf_op jit(solution)/shard_map/reduce_scatter | solution.py:24
  75.6 1.7 bitcast_dynamic-update-slice_fusion.5
  78.0 3.7 all-to-all-start.1
  82.0 5.1 %all-to-all-done.1 = bf16[4,128,256]{2,1,0:T(8,128)(2,1)S(1)} async-done(((bf16[4,128,256]{2,1,0:T(8,128)(2,1)}), bf16[4,128,256]{2,1,0:T(8,128)(2,1)S(1)}, u32[]{:S(2)}, u32[]{:S(2)}) %all-to-all-start.1) | async-done | bytes 262176 | tf_op jit(solution)/shard_map/all_to_all | solution.py:9
  87.9 5.3 %fusion.38 = f32[50,128,256]{1,2,0:T(8,128)} fusion(bf16[50,128,256]{2,1,0:T(8,128)(2,1)S(1)} %gather_fusion.1, pred[50]{0:T(512)(128)(4,1)} %get-tuple-element.33, bf16[7,1,50,128,128]{4,3,2,1,0:T(8,128)(2,1)} %param.9), kind=kOutput, calls=%fused_computation.50 | convolution fusion | flops 421068800 | bytes 11469312 | tf_op jit(solution)/shard_map/qab,qbc->qac/dot_general | solution.py:15
  93.2 8.2 %copy.61 = f32[50,128,256]{2,1,0:T(8,128)} copy(f32[50,128,256]{1,2,0:T(8,128)} %fusion.38) | data formatting | bytes 13107200 | tf_op jit(solution)/shard_map/qab,qbc->qac/dot_general | solution.py:15
  101.4 3.3 slice_bitcast_fusion.5
  104.7 6.1 %fusion.80 = bf16[8,128,256]{2,0,1:T(8,128)(2,1)S(1)} fusion(f32[128,256,50]{1,0,2:T(8,128)S(1)} %slice_bitcast_fusion.5, s32[50]{0:T(128)S(1)} %copy-done.2), kind=kOutput, calls=%fused_computation.78 | convolution fusion | flops 157548944 | bytes 7078088 | tf_op jit(solution)/shard_map/dot_general | solution.py:17
  110.8 0.9 copy.63
  111.7 28.9 %reduce-scatter.10.cloned.1.call-done = bf16[1,128,256]{2,1,0:T(8,128)(2,1)} async-done(((bf16[8,128,256]{2,1,0:T(8,128)(2,1)}), bf16[1,128,256]{2,1,0:T(8,128)(2,1)}) %reduce-scatter.10.cloned.1.call-update) | async-done | bytes 65552 | tf_op jit(solution)/shard_map/reduce_scatter | solution.py:24
  140.6 1.7 bitcast_dynamic-update-slice_fusion.4
  143.0 3.8 all-to-all-start.2
  147.2 4.9 %all-to-all-done.2 = bf16[4,128,256]{2,1,0:T(8,128)(2,1)S(1)} async-done(((bf16[4,128,256]{2,1,0:T(8,128)(2,1)}), bf16[4,128,256]{2,1,0:T(8,128)(2,1)S(1)}, u32[]{:S(2)}, u32[]{:S(2)}) %all-to-all-start.2) | async-done | bytes 262176 | tf_op jit(solution)/shard_map/all_to_all | solution.py:9
  152.9 5.3 %fusion.41 = f32[50,128,256]{1,2,0:T(8,128)} fusion(bf16[50,128,256]{2,1,0:T(8,128)(2,1)S(1)} %gather_fusion.2, pred[50]{0:T(512)(128)(4,1)} %get-tuple-element.31, bf16[7,1,50,128,128]{4,3,2,1,0:T(8,128)(2,1)} %param.9), kind=kOutput, calls=%fused_computation.51 | convolution fusion | flops 421068800 | bytes 11469312 | tf_op jit(solution)/shard_map/qab,qbc->qac/dot_general | solution.py:15
  158.2 8.2 %copy.66 = f32[50,128,256]{2,1,0:T(8,128)} copy(f32[50,128,256]{1,2,0:T(8,128)} %fusion.41) | data formatting | bytes 13107200 | tf_op jit(solution)/shard_map/qab,qbc->qac/dot_general | solution.py:15
  166.4 3.3 slice_bitcast_fusion.4
  169.8 6.1 %fusion.83 = bf16[8,128,256]{2,0,1:T(8,128)(2,1)S(1)} fusion(f32[128,256,50]{1,0,2:T(8,128)S(1)} %slice_bitcast_fusion.4, s32[50]{0:T(128)S(1)} %copy-done.1), kind=kOutput, calls=%fused_computation.79 | convolution fusion | flops 157548944 | bytes 7078088 | tf_op jit(solution)/shard_map/dot_general | solution.py:17
  176.8 28.9 %reduce-scatter.12.cloned.1.call-done = bf16[1,128,256]{2,1,0:T(8,128)(2,1)} async-done(((bf16[8,128,256]{2,1,0:T(8,128)(2,1)}), bf16[1,128,256]{2,1,0:T(8,128)(2,1)}) %reduce-scatter.12.cloned.1.call-update) | async-done | bytes 65552 | tf_op jit(solution)/shard_map/reduce_scatter | solution.py:24
  205.6 1.7 bitcast_dynamic-update-slice_fusion.3
  208.0 3.6 all-to-all-start.3
  211.8 5.2 %all-to-all-done.3 = bf16[4,128,256]{2,1,0:T(8,128)(2,1)S(1)} async-done(((bf16[4,128,256]{2,1,0:T(8,128)(2,1)}), bf16[4,128,256]{2,1,0:T(8,128)(2,1)S(1)}, u32[]{:S(2)}, u32[]{:S(2)}) %all-to-all-start.3) | async-done | bytes 262176 | tf_op jit(solution)/shard_map/all_to_all | solution.py:9
  217.8 5.3 %fusion.44 = f32[50,128,256]{1,2,0:T(8,128)} fusion(bf16[50,128,256]{2,1,0:T(8,128)(2,1)S(1)} %gather_fusion.3, pred[50]{0:T(512)(128)(4,1)} %get-tuple-element.29, bf16[7,1,50,128,128]{4,3,2,1,0:T(8,128)(2,1)} %param.9), kind=kOutput, calls=%fused_computation.52 | convolution fusion | flops 421068800 | bytes 11469312 | tf_op jit(solution)/shard_map/qab,qbc->qac/dot_general | solution.py:15
  223.1 8.2 %copy.71 = f32[50,128,256]{2,1,0:T(8,128)} copy(f32[50,128,256]{1,2,0:T(8,128)} %fusion.44) | data formatting | bytes 13107200 | tf_op jit(solution)/shard_map/qab,qbc->qac/dot_general | solution.py:15
  231.3 3.3 slice_bitcast_fusion.3
  234.6 6.1 %fusion.86 = bf16[8,128,256]{2,0,1:T(8,128)(2,1)S(1)} fusion(f32[128,256,50]{1,0,2:T(8,128)S(1)} %slice_bitcast_fusion.3, s32[50]{0:T(128)S(1)} %copy-done), kind=kOutput, calls=%fused_computation.80 | convolution fusion | flops 157548944 | bytes 7078088 | tf_op jit(solution)/shard_map/dot_general | solution.py:17
  240.7 0.9 copy.73
  241.6 29.1 %reduce-scatter.14.cloned.1.call-done = bf16[1,128,256]{2,1,0:T(8,128)(2,1)} async-done(((bf16[8,128,256]{2,1,0:T(8,128)(2,1)}), bf16[1,128,256]{2,1,0:T(8,128)(2,1)}) %reduce-scatter.14.cloned.1.call-update) | async-done | bytes 65552 | tf_op jit(solution)/shard_map/reduce_scatter | solution.py:24
  270.7 1.7 bitcast_dynamic-update-slice_fusion.2
  273.1 3.5 all-to-all-start.4
  276.9 5.1 %all-to-all-done.4 = bf16[4,128,256]{2,1,0:T(8,128)(2,1)S(1)} async-done(((bf16[4,128,256]{2,1,0:T(8,128)(2,1)}), bf16[4,128,256]{2,1,0:T(8,128)(2,1)S(1)}, u32[]{:S(2)}, u32[]{:S(2)}) %all-to-all-start.4) | async-done | bytes 262176 | tf_op jit(solution)/shard_map/all_to_all | solution.py:9
  282.8 5.3 %fusion.47 = f32[50,128,256]{1,2,0:T(8,128)} fusion(bf16[50,128,256]{2,1,0:T(8,128)(2,1)S(1)} %gather_fusion.4, pred[50]{0:T(512)(128)(4,1)} %get-tuple-element.27, bf16[7,1,50,128,128]{4,3,2,1,0:T(8,128)(2,1)} %param.9), kind=kOutput, calls=%fused_computation.53 | convolution fusion | flops 421068800 | bytes 11469312 | tf_op jit(solution)/shard_map/qab,qbc->qac/dot_general | solution.py:15
  288.1 8.2 %copy.76 = f32[50,128,256]{2,1,0:T(8,128)} copy(f32[50,128,256]{1,2,0:T(8,128)} %fusion.47) | data formatting | bytes 13107200 | tf_op jit(solution)/shard_map/qab,qbc->qac/dot_general | solution.py:15
  296.3 3.3 slice_bitcast_fusion.2
  299.6 6.1 %fusion.89 = bf16[8,128,256]{2,0,1:T(8,128)(2,1)S(1)} fusion(f32[128,256,50]{1,0,2:T(8,128)S(1)} %slice_bitcast_fusion.2, s32[50]{0:T(128)S(1)} %get-tuple-element.21), kind=kOutput, calls=%fused_computation.81 | convolution fusion | flops 157548944 | bytes 7078088 | tf_op jit(solution)/shard_map/dot_general | solution.py:17
  305.7 0.9 copy.78
  306.7 29.0 %reduce-scatter.16.cloned.1.call-done = bf16[1,128,256]{2,1,0:T(8,128)(2,1)} async-done(((bf16[8,128,256]{2,1,0:T(8,128)(2,1)}), bf16[1,128,256]{2,1,0:T(8,128)(2,1)}) %reduce-scatter.16.cloned.1.call-update) | async-done | bytes 65552 | tf_op jit(solution)/shard_map/reduce_scatter | solution.py:24
  335.7 1.7 bitcast_dynamic-update-slice_fusion.1
  338.1 3.7 all-to-all-start.5
  342.0 5.1 %all-to-all-done.5 = bf16[4,128,256]{2,1,0:T(8,128)(2,1)S(1)} async-done(((bf16[4,128,256]{2,1,0:T(8,128)(2,1)}), bf16[4,128,256]{2,1,0:T(8,128)(2,1)S(1)}, u32[]{:S(2)}, u32[]{:S(2)}) %all-to-all-start.5) | async-done | bytes 262176 | tf_op jit(solution)/shard_map/all_to_all | solution.py:9
  347.9 5.3 %fusion.50 = f32[50,128,256]{1,2,0:T(8,128)} fusion(bf16[50,128,256]{2,1,0:T(8,128)(2,1)S(1)} %gather_fusion.5, pred[50]{0:T(512)(128)(4,1)S(1)} %copy-done.5, bf16[7,1,50,128,128]{4,3,2,1,0:T(8,128)(2,1)} %param.9), kind=kOutput, calls=%fused_computation.54 | convolution fusion | flops 421068800 | bytes 11468850 | tf_op jit(solution)/shard_map/qab,qbc->qac/dot_general | solution.py:15
  353.2 8.2 %copy.81 = f32[50,128,256]{2,1,0:T(8,128)} copy(f32[50,128,256]{1,2,0:T(8,128)} %fusion.50) | data formatting | bytes 13107200 | tf_op jit(solution)/shard_map/qab,qbc->qac/dot_general | solution.py:15
  361.4 3.3 slice_bitcast_fusion.1
  364.7 6.1 %fusion.92 = bf16[8,128,256]{2,0,1:T(8,128)(2,1)S(1)} fusion(f32[128,256,50]{1,0,2:T(8,128)S(1)} %slice_bitcast_fusion.1, s32[50]{0:T(128)S(1)} %get-tuple-element.26), kind=kOutput, calls=%fused_computation.82 | convolution fusion | flops 157548944 | bytes 7078088 | tf_op jit(solution)/shard_map/dot_general | solution.py:17
  370.9 0.9 copy.83
  371.8 28.9 %reduce-scatter.18.cloned.1.call-done = bf16[1,128,256]{2,1,0:T(8,128)(2,1)} async-done(((bf16[8,128,256]{2,1,0:T(8,128)(2,1)}), bf16[1,128,256]{2,1,0:T(8,128)(2,1)}) %reduce-scatter.18.cloned.1.call-update) | async-done | bytes 65552 | tf_op jit(solution)/shard_map/reduce_scatter | solution.py:24
  400.7 1.7 bitcast_dynamic-update-slice_fusion
  403.1 3.7 all-to-all-start.6
  407.1 5.1 %all-to-all-done.6 = bf16[4,128,256]{2,1,0:T(8,128)(2,1)S(1)} async-done(((bf16[4,128,256]{2,1,0:T(8,128)(2,1)}), bf16[4,128,256]{2,1,0:T(8,128)(2,1)S(1)}, u32[]{:S(2)}, u32[]{:S(2)}) %all-to-all-start.6) | async-done | bytes 262176 | tf_op jit(solution)/shard_map/all_to_all | solution.py:9
  413.0 5.3 %fusion.53 = f32[50,128,256]{1,2,0:T(8,128)} fusion(bf16[50,128,256]{2,1,0:T(8,128)(2,1)S(1)} %gather_fusion.6, pred[50]{0:T(512)(128)(4,1)S(1)} %copy-done.4, bf16[7,1,50,128,128]{4,3,2,1,0:T(8,128)(2,1)} %param.9), kind=kOutput, calls=%fused_computation.55 | convolution fusion | flops 421068800 | bytes 11468850 | tf_op jit(solution)/shard_map/qab,qbc->qac/dot_general | solution.py:15
  418.3 8.2 %copy.86 = f32[50,128,256]{2,1,0:T(8,128)} copy(f32[50,128,256]{1,2,0:T(8,128)} %fusion.53) | data formatting | bytes 13107200 | tf_op jit(solution)/shard_map/qab,qbc->qac/dot_general | solution.py:15
  426.5 3.3 slice_bitcast_fusion
  429.8 6.1 %fusion.95 = bf16[8,128,256]{2,0,1:T(8,128)(2,1)S(1)} fusion(f32[128,256,50]{1,0,2:T(8,128)S(1)} %slice_bitcast_fusion, s32[50]{0:T(128)S(1)} %get-tuple-element.20), kind=kOutput, calls=%fused_computation.83 | convolution fusion | flops 157548944 | bytes 7078088 | tf_op jit(solution)/shard_map/dot_general | solution.py:17
  436.8 28.8 %reduce-scatter.20.cloned.1.call-done = bf16[1,128,256]{2,1,0:T(8,128)(2,1)} async-done(((bf16[8,128,256]{2,1,0:T(8,128)(2,1)}), bf16[1,128,256]{2,1,0:T(8,128)(2,1)}) %reduce-scatter.20.cloned.1.call-update) | async-done | bytes 65552 | tf_op jit(solution)/shard_map/reduce_scatter | solution.py:24
  465.6 1.7 fusion.98
  (61 shorter events, 13.7 us)
Async XLA Ops:
  8.9 10.6 %all-to-all-start = ((bf16[4,128,256]{2,1,0:T(8,128)(2,1)}), bf16[4,128,256]{2,1,0:T(8,128)(2,1)S(1)}, u32[]{:S(2)}, u32[]{:S(2)}) async-start(bf16[4,128,256]{2,1,0:T(8,128)(2,1)} %concatenate.21), calls=%async_computation | async-start | bytes 524288 | tf_op jit(solution)/shard_map/all_to_all | solution.py:9
  14.1 61.5 %reduce-scatter.8.cloned.1.call-start = ((), (), s32[]{:S(2)}) async-start(), calls=%async_computation.14 | async-start | bytes 589824 | tf_op jit(solution)/shard_map/reduce_scatter | solution.py:24
  33.8 3.3 copy-start.3
  37.1 44.9 %copy-start.11 = (s32[50]{0:T(128)S(1)}, s32[50]{0:T(128)}, u32[]{:S(2)}) copy-start(s32[50]{0:T(128)} %get-tuple-element.34) | copy-start | bytes 604
  78.0 9.1 %all-to-all-start.1 = ((bf16[4,128,256]{2,1,0:T(8,128)(2,1)}), bf16[4,128,256]{2,1,0:T(8,128)(2,1)S(1)}, u32[]{:S(2)}, u32[]{:S(2)}) async-start(bf16[4,128,256]{2,1,0:T(8,128)(2,1)} %concatenate.22), calls=%async_computation.2 | async-start | bytes 524288 | tf_op jit(solution)/shard_map/all_to_all | solution.py:9
  81.8 58.8 %reduce-scatter.10.cloned.1.call-start = ((), (), s32[]{:S(2)}) async-start(), calls=%async_computation.15 | async-start | bytes 589824 | tf_op jit(solution)/shard_map/reduce_scatter | solution.py:24
  101.4 3.3 copy-start.2
  104.7 42.5 %copy-start.10 = (s32[50]{0:T(128)S(1)}, s32[50]{0:T(128)}, u32[]{:S(2)}) copy-start(s32[50]{0:T(128)} %get-tuple-element.32) | copy-start | bytes 604
  143.0 9.1 %all-to-all-start.2 = ((bf16[4,128,256]{2,1,0:T(8,128)(2,1)}), bf16[4,128,256]{2,1,0:T(8,128)(2,1)S(1)}, u32[]{:S(2)}, u32[]{:S(2)}) async-start(bf16[4,128,256]{2,1,0:T(8,128)(2,1)} %concatenate.23), calls=%async_computation.4 | async-start | bytes 524288 | tf_op jit(solution)/shard_map/all_to_all | solution.py:9
  146.8 58.8 %reduce-scatter.12.cloned.1.call-start = ((), (), s32[]{:S(2)}) async-start(), calls=%async_computation.16 | async-start | bytes 589824 | tf_op jit(solution)/shard_map/reduce_scatter | solution.py:24
  166.4 3.3 copy-start.1
  169.7 42.1 %copy-start.9 = (s32[50]{0:T(128)S(1)}, s32[50]{0:T(128)}, u32[]{:S(2)}) copy-start(s32[50]{0:T(128)} %get-tuple-element.30) | copy-start | bytes 604
  208.0 9.0 %all-to-all-start.3 = ((bf16[4,128,256]{2,1,0:T(8,128)(2,1)}), bf16[4,128,256]{2,1,0:T(8,128)(2,1)S(1)}, u32[]{:S(2)}, u32[]{:S(2)}) async-start(bf16[4,128,256]{2,1,0:T(8,128)(2,1)} %concatenate.24), calls=%async_computation.6 | async-start | bytes 524288 | tf_op jit(solution)/shard_map/all_to_all | solution.py:9
  211.6 59.1 %reduce-scatter.14.cloned.1.call-start = ((), (), s32[]{:S(2)}) async-start(), calls=%async_computation.17 | async-start | bytes 589824 | tf_op jit(solution)/shard_map/reduce_scatter | solution.py:24
  231.3 3.3 copy-start
  234.6 42.3 %copy-start.8 = (s32[50]{0:T(128)S(1)}, s32[50]{0:T(128)}, u32[]{:S(2)}) copy-start(s32[50]{0:T(128)} %get-tuple-element.28) | copy-start | bytes 604
  273.1 8.9 %all-to-all-start.4 = ((bf16[4,128,256]{2,1,0:T(8,128)(2,1)}), bf16[4,128,256]{2,1,0:T(8,128)(2,1)S(1)}, u32[]{:S(2)}, u32[]{:S(2)}) async-start(bf16[4,128,256]{2,1,0:T(8,128)(2,1)} %concatenate.25), calls=%async_computation.8 | async-start | bytes 524288 | tf_op jit(solution)/shard_map/all_to_all | solution.py:9
  276.7 59.0 %reduce-scatter.16.cloned.1.call-start = ((), (), s32[]{:S(2)}) async-start(), calls=%async_computation.18 | async-start | bytes 589824 | tf_op jit(solution)/shard_map/reduce_scatter | solution.py:24
  299.6 42.4 %copy-start.7 = (s32[50]{0:T(128)S(1)}, s32[50]{0:T(128)}, u32[]{:S(2)}) copy-start(s32[50]{0:T(128)} %get-tuple-element.38) | copy-start | bytes 604
  305.7 42.2 %copy-start.5 = (pred[50]{0:T(512)(128)(4,1)S(1)}, pred[50]{0:T(512)(128)(4,1)}, u32[]{:S(2)}) copy-start(pred[50]{0:T(512)(128)(4,1)} %get-tuple-element.37) | copy-start | bytes 154
  338.1 9.0 %all-to-all-start.5 = ((bf16[4,128,256]{2,1,0:T(8,128)(2,1)}), bf16[4,128,256]{2,1,0:T(8,128)(2,1)S(1)}, u32[]{:S(2)}, u32[]{:S(2)}) async-start(bf16[4,128,256]{2,1,0:T(8,128)(2,1)} %concatenate.26), calls=%async_computation.10 | async-start | bytes 524288 | tf_op jit(solution)/shard_map/all_to_all | solution.py:9
  341.8 58.9 %reduce-scatter.18.cloned.1.call-start = ((), (), s32[]{:S(2)}) async-start(), calls=%async_computation.19 | async-start | bytes 589824 | tf_op jit(solution)/shard_map/reduce_scatter | solution.py:24
  364.7 42.4 %copy-start.6 = (s32[50]{0:T(128)S(1)}, s32[50]{0:T(128)}, u32[]{:S(2)}) copy-start(s32[50]{0:T(128)} %get-tuple-element.7) | copy-start | bytes 604
  370.8 42.1 %copy-start.4 = (pred[50]{0:T(512)(128)(4,1)S(1)}, pred[50]{0:T(512)(128)(4,1)}, u32[]{:S(2)}) copy-start(pred[50]{0:T(512)(128)(4,1)} %get-tuple-element.6) | copy-start | bytes 154
  403.1 9.1 %all-to-all-start.6 = ((bf16[4,128,256]{2,1,0:T(8,128)(2,1)}), bf16[4,128,256]{2,1,0:T(8,128)(2,1)S(1)}, u32[]{:S(2)}, u32[]{:S(2)}) async-start(bf16[4,128,256]{2,1,0:T(8,128)(2,1)} %concatenate.27), calls=%async_computation.12 | async-start | bytes 524288 | tf_op jit(solution)/shard_map/all_to_all | solution.py:9
  406.8 58.7 %reduce-scatter.20.cloned.1.call-start = ((), (), s32[]{:S(2)}) async-start(), calls=%async_computation.20 | async-start | bytes 589824 | tf_op jit(solution)/shard_map/reduce_scatter | solution.py:24
Sparse Core Ops, SparseCore 0:
  44.2 31.3 reduce-scatter.7
  111.9 28.6 reduce-scatter.9
  176.9 28.6 reduce-scatter.11
  241.8 28.9 reduce-scatter.13
  306.8 28.8 reduce-scatter.15
  371.9 28.7 reduce-scatter.17
  436.9 28.6 reduce-scatter.19
